TPU v7x, 128 devices: a whole 4x4x4 slice. The times are simulated.
128 devices in a mesh: dap: 16 (over z, y), dp: 8 (over x, core).
Axes of the slice: x: 4, y: 4, z: 4, core: 2. Of those that a mesh axis runs over, the one named last changes fastest.
Arguments:
- pair_z: bfloat16 [32, 128, 128, 128], P('dp', 'dap')
- single_s: bfloat16 [32, 128, 384], P('dp', 'dap')
- token_mask: int32 [32, 128], P('dp')
- dz_out: bfloat16 [32, 128, 128, 128], P('dp', 'dap')
- ds_out: bfloat16 [32, 128, 384], P('dp', 'dap')
- w_pa: bfloat16 [128, 512], replicated
- w_pb: bfloat16 [128, 512], replicated
- w_po: bfloat16 [512, 128], replicated
- w_bias: bfloat16 [128, 16], replicated
- w_q: bfloat16 [384, 384], replicated
- q_bias: bfloat16 [384], replicated
- w_kv: bfloat16 [384, 768], replicated
- w_g: bfloat16 [384, 384], replicated
- w_o: bfloat16 [384, 384], replicated
- w_sa: bfloat16 [384, 1536], replicated
- w_sb: bfloat16 [384, 1536], replicated
- w_so: bfloat16 [1536, 384], replicated
Outputs:
- output 1: bfloat16 [32, 128, 128, 128], P('dp', 'dap')
- output 2: bfloat16 [32, 128, 384], P('dp', 'dap')
- output 3: float32 [128, 512], replicated
- output 4: float32 [128, 512], replicated
- output 5: float32 [512, 128], replicated
- output 6: float32 [128, 16], replicated
- output 7: float32 [384, 384], replicated
- output 8: float32 [384], replicated
- output 9: float32 [384, 768], replicated
- output 10: float32 [384, 384], replicated
- output 11: float32 [384, 384], replicated
- output 12: float32 [384, 1536], replicated
- output 13: float32 [384, 1536], replicated
- output 14: float32 [1536, 384], replicated
All inputs are finite; a program needn't handle non-finite values.
Results may differ from a plain program's by a relative error of at most 0.02.
Values are sent between devices in bfloat16 or wider.
A program may use at most 1 GiB of HBM per device.

v0:
```python
import math
import jax
import jax.numpy as jnp
from jax import lax
from jax.sharding import PartitionSpec as P

HEAD_DIM = 24
EPSILON = 1e-5
MASK_BIG = 1e9


def contract(equation, left_op, right_op):
    return jnp.einsum(equation, left_op, right_op, preferred_element_type=jnp.float32)


def layer_norm(values):
    wide_vals = values.astype(jnp.float32)
    centred = wide_vals - jnp.mean(wide_vals, axis=-1, keepdims=True)
    inv_std = lax.rsqrt(jnp.mean(centred * centred, axis=-1, keepdims=True) + EPSILON)
    return centred * inv_std, inv_std


def norm_grad(normed, inv_std, grad_out):
    mean_grad = jnp.mean(grad_out, axis=-1, keepdims=True)
    mean_proj = jnp.mean(grad_out * normed, axis=-1, keepdims=True)
    return inv_std * (grad_out - mean_grad - normed * mean_proj)


def swiglu_grad(hid_a, hid_b, grad_hidden):
    sig_a = jax.nn.sigmoid(hid_a)
    grad_a = grad_hidden * hid_b * sig_a * (1.0 + hid_a * (1.0 - sig_a))
    return grad_a, grad_hidden * hid_a * sig_a


def pair_forward(z_rows, w_pa, w_pb, w_po, w_bias):
    normed, _ = layer_norm(z_rows)
    normed_bf = normed.astype(jnp.bfloat16)
    hid_a = contract('rjc,cf->rjf', normed_bf, w_pa)
    hid_b = contract('rjc,cf->rjf', normed_bf, w_pb)
    hidden = (jax.nn.silu(hid_a) * hid_b).astype(jnp.bfloat16)
    z_new = (z_rows.astype(jnp.float32) + contract('rjf,fc->rjc', hidden, w_po)).astype(jnp.bfloat16)
    bias_norm, _ = layer_norm(z_new)
    return z_new, contract('rjc,ch->rjh', bias_norm.astype(jnp.bfloat16), w_bias)


def pair_backward(z_rows, new_rows, dz_rows, bias_grad, w_pa, w_pb, w_po, w_bias):
    bias_norm, bias_inv = layer_norm(new_rows)
    d_w_bias = contract('rjc,rjh->ch', bias_norm.astype(jnp.bfloat16), bias_grad)
    grad_norm = contract('rjh,ch->rjc', bias_grad, w_bias)
    grad_new = dz_rows.astype(jnp.float32) + norm_grad(bias_norm, bias_inv, grad_norm)
    grad_new_bf = grad_new.astype(jnp.bfloat16)
    normed, inv_std = layer_norm(z_rows)
    normed_bf = normed.astype(jnp.bfloat16)
    hid_a = contract('rjc,cf->rjf', normed_bf, w_pa)
    hid_b = contract('rjc,cf->rjf', normed_bf, w_pb)
    hidden = (jax.nn.silu(hid_a) * hid_b).astype(jnp.bfloat16)
    d_w_po = contract('rjf,rjc->fc', hidden, grad_new_bf)
    grad_hidden = contract('rjc,fc->rjf', grad_new_bf, w_po)
    grad_a, grad_b = swiglu_grad(hid_a, hid_b, grad_hidden)
    grad_a = grad_a.astype(jnp.bfloat16)
    grad_b = grad_b.astype(jnp.bfloat16)
    d_w_pa = contract('rjc,rjf->cf', normed_bf, grad_a)
    d_w_pb = contract('rjc,rjf->cf', normed_bf, grad_b)
    grad_normed = contract('rjf,cf->rjc', grad_a, w_pa) + contract('rjf,cf->rjc', grad_b, w_pb)
    dz_in = (grad_new + norm_grad(normed, inv_std, grad_normed)).astype(jnp.bfloat16)
    return dz_in, (d_w_pa, d_w_pb, d_w_po, d_w_bias)


def solution(mesh):
    pair_spec = P('dp', 'dap', None, None)
    single_spec = P('dp', 'dap', None)

    def body(pair_z, single_s, token_mask, dz_out, ds_out, w_pa, w_pb, w_po, w_bias, w_q, q_bias, w_kv, w_g, w_o, w_sa, w_sb, w_so):
        num_cplx, num_rows, num_tok, pair_dim = pair_z.shape
        attn_width = w_q.shape[1]
        num_heads = attn_width // HEAD_DIM
        row_group = math.gcd(num_rows, 16)
        num_blocks = num_cplx * num_rows // row_group
        logit_scale = HEAD_DIM ** -0.5
        z_blocks = pair_z.reshape(num_blocks, row_group, num_tok, pair_dim)

        def forward_rows(z_rows):
            return pair_forward(z_rows, w_pa, w_pb, w_po, w_bias)

        z_new, bias_rows = lax.map(forward_rows, z_blocks)
        pair_bias = jnp.transpose(bias_rows.reshape(num_cplx, num_rows, num_tok, num_heads), (0, 3, 1, 2))

        s_norm, s_inv = layer_norm(single_s)
        act_norm = s_norm.astype(jnp.bfloat16)
        queries = (contract('bic,ce->bie', act_norm, w_q) + q_bias.astype(jnp.float32)).astype(jnp.bfloat16)
        kv_local = contract('bic,ce->bie', act_norm, w_kv).astype(jnp.bfloat16)
        gate_vals = jax.nn.sigmoid(contract('bic,ce->bie', act_norm, w_g))
        kv_all = lax.all_gather(kv_local, 'dap', axis=1, tiled=True)
        key_heads = kv_all[:, :, :attn_width].reshape(num_cplx, num_tok, num_heads, HEAD_DIM)
        value_heads = kv_all[:, :, attn_width:].reshape(num_cplx, num_tok, num_heads, HEAD_DIM)
        query_heads = queries.reshape(num_cplx, num_rows, num_heads, HEAD_DIM)
        key_mask = MASK_BIG * (token_mask.astype(jnp.float32) - 1.0)
        logits = contract('bihd,bjhd->bhij', query_heads, key_heads) * logit_scale + pair_bias + key_mask[:, None, None, :]
        attn_prob = jax.nn.softmax(logits, axis=-1)
        prob_bf = attn_prob.astype(jnp.bfloat16)
        attended = contract('bhij,bjhd->bihd', prob_bf, value_heads).reshape(num_cplx, num_rows, attn_width)
        gated = (gate_vals * attended).astype(jnp.bfloat16)
        s_mid = (single_s.astype(jnp.float32) + contract('bie,ec->bic', gated, w_o)).astype(jnp.bfloat16)
        mid_norm, mid_inv = layer_norm(s_mid)
        mid_act = mid_norm.astype(jnp.bfloat16)
        trans_a = contract('bic,cf->bif', mid_act, w_sa)
        trans_b = contract('bic,cf->bif', mid_act, w_sb)
        trans_hidden = (jax.nn.silu(trans_a) * trans_b).astype(jnp.bfloat16)

        d_w_so = contract('bif,bic->fc', trans_hidden, ds_out)
        grad_hidden = contract('bic,fc->bif', ds_out, w_so)
        grad_ta, grad_tb = swiglu_grad(trans_a, trans_b, grad_hidden)
        grad_ta = grad_ta.astype(jnp.bfloat16)
        grad_tb = grad_tb.astype(jnp.bfloat16)
        d_w_sa = contract('bic,bif->cf', mid_act, grad_ta)
        d_w_sb = contract('bic,bif->cf', mid_act, grad_tb)
        grad_mid_norm = contract('bif,cf->bic', grad_ta, w_sa) + contract('bif,cf->bic', grad_tb, w_sb)
        grad_mid = ds_out.astype(jnp.float32) + norm_grad(mid_norm, mid_inv, grad_mid_norm)
        grad_mid_bf = grad_mid.astype(jnp.bfloat16)
        d_w_o = contract('bie,bic->ec', gated, grad_mid_bf)
        grad_gated = contract('bic,ec->bie', grad_mid_bf, w_o)
        grad_gate_pre = (grad_gated * attended * gate_vals * (1.0 - gate_vals)).astype(jnp.bfloat16)
        grad_att = (grad_gated * gate_vals).astype(jnp.bfloat16).reshape(num_cplx, num_rows, num_heads, HEAD_DIM)
        grad_prob = contract('bihd,bjhd->bhij', grad_att, value_heads)
        grad_values = contract('bhij,bihd->bjhd', prob_bf, grad_att)
        grad_logits = attn_prob * (grad_prob - jnp.sum(attn_prob * grad_prob, axis=-1, keepdims=True))
        grad_logits_bf = grad_logits.astype(jnp.bfloat16)
        grad_query = contract('bhij,bjhd->bihd', grad_logits_bf, key_heads) * logit_scale
        grad_keys = contract('bhij,bihd->bjhd', grad_logits_bf, query_heads) * logit_scale
        grad_kv_part = jnp.concatenate([grad_keys.reshape(num_cplx, num_tok, attn_width), grad_values.reshape(num_cplx, num_tok, attn_width)], axis=-1).astype(jnp.bfloat16)
        grad_kv = lax.psum_scatter(grad_kv_part, 'dap', scatter_dimension=1, tiled=True)
        grad_query_bf = grad_query.reshape(num_cplx, num_rows, attn_width).astype(jnp.bfloat16)
        d_w_q = contract('bic,bie->ce', act_norm, grad_query_bf)
        d_q_bias = jnp.sum(grad_query, axis=(0, 1)).reshape(attn_width)
        d_w_kv = contract('bic,bie->ce', act_norm, grad_kv)
        d_w_g = contract('bic,bie->ce', act_norm, grad_gate_pre)
        grad_act = contract('bie,ce->bic', grad_query_bf, w_q) + contract('bie,ce->bic', grad_kv, w_kv) + contract('bie,ce->bic', grad_gate_pre, w_g)
        ds_in = (grad_mid + norm_grad(s_norm, s_inv, grad_act)).astype(jnp.bfloat16)

        grad_bias = jnp.transpose(grad_logits_bf, (0, 2, 3, 1)).reshape(num_blocks, row_group, num_tok, num_heads)
        dz_blocks = dz_out.reshape(num_blocks, row_group, num_tok, pair_dim)

        def backward_rows(running, block_in):
            z_rows, new_rows, dz_rows, bias_grad = block_in
            dz_rows_in, row_grads = pair_backward(z_rows, new_rows, dz_rows, bias_grad, w_pa, w_pb, w_po, w_bias)
            return tuple(acc_sum + update for acc_sum, update in zip(running, row_grads)), dz_rows_in

        zero_grads = (jnp.zeros(w_pa.shape, jnp.float32), jnp.zeros(w_pb.shape, jnp.float32), jnp.zeros(w_po.shape, jnp.float32), jnp.zeros(w_bias.shape, jnp.float32))
        pair_grads, dz_in = lax.scan(backward_rows, zero_grads, (z_blocks, z_new, dz_blocks, grad_bias))
        weight_grads = lax.psum(pair_grads + (d_w_q, d_q_bias, d_w_kv, d_w_g, d_w_o, d_w_sa, d_w_sb, d_w_so), ('dap', 'dp'))
        return (dz_in.reshape(num_cplx, num_rows, num_tok, pair_dim), ds_in) + weight_grads

    in_specs = (pair_spec, single_spec, P('dp', None), pair_spec, single_spec) + (P(),) * 12
    out_specs = (pair_spec, single_spec) + (P(),) * 12
    return jax.shard_map(body, mesh=mesh, in_specs=in_specs, out_specs=out_specs, check_vma=False)
```

profile of v0, /device:TPU:1, one launch (start us, length us, event | category | flops | bytes accessed | tf_op | source)
XLA Modules:
  0.0 406.6 jit_solution(1698167031643525211)
XLA Ops:
  16.1 21.7 %all_gather.3 = bf16[4,128,768]{2,1,0:T(8,128)(2,1)S(1)} all-gather(bf16[4,8,768]{2,1,0:T(8,128)(2,1)S(1)} %convolution_convert_fusion.1), channel_id=1, replica_groups=mesh['dap'=16,'dp'=8] {'dap'}, dimensions={1}, use_global_device_ids=true | all-gather | bytes 835584 | tf_op jit(solution)/shard_map/all_gather | solution.py:93
  38.7 2.0 copy.95
  43.2 36.5 %while.31 = (s32[]{:T(128)}, bf16[4,8,128,128]{2,3,1,0:T(8,128)(2,1)S(1)}, f32[4,8,128,16]{2,1,3,0:T(8,128)}, bf16[4,8,128,128]{2,3,1,0:T(8,128)(2,1)S(1)}, bf16...) while((s32[]{:T(128)}, ...), condition=%wide.region_5.6_spmd, body=%wide.region_0.5_spmd.sunk | while | flops 413534208 | bytes 7492725 | solution.py:85
  45.2 3.3 bitcast_dynamic-update-slice_fusion.2
  54.3 3.3 bitcast_dynamic-update-slice_fusion.2
  63.4 3.3 bitcast_dynamic-update-slice_fusion.2
  72.6 3.3 bitcast_dynamic-update-slice_fusion.2
  79.7 2.1 fusion.170
  95.4 2.7 multiply_reduce_fusion
  98.1 2.3 convolution_convert_fusion
  100.4 1.9 copy.109
  104.3 2.1 fusion.89
  106.4 1.9 copy.108
  108.3 2.1 pad_maximum_fusion
  110.7 2.6 fusion.177
  113.3 2.1 fusion.123
  115.4 79.0 %while.32 = (s32[]{:T(128)}, f32[128,512]{1,0:T(8,128)}, f32[128,512]{1,0:T(8,128)}, f32[512,128]{1,0:T(8,128)}, f32[128,16]{0,1:T(8,128)}, /*index=5*/bf16[4,8,...) while((s32[]{:T(128)}, f32[128,512]{1,0:T(8,128)}, ...), condition=%wide.region_24.25_spmd.clone, body=%wide.region_15.24_spmd.clone.sunk | while | flops 1101010944 | bytes 37573000 | solution.py:149
  119.5 1.8 copy.165
  138.7 1.8 copy.165
  143.7 2.5 fusion.270
  158.9 1.8 copy.165
  163.8 2.5 fusion.270
  184.0 2.5 fusion.270
  195.6 1.9 convolution_bitcast_fusion.11
  197.5 1.9 convolution_bitcast_fusion.9
  201.9 1.9 convolution_bitcast_fusion.6
  203.8 1.9 convolution_bitcast_fusion.7
  205.7 1.9 convolution_bitcast_fusion.5
  207.7 2.2 convolution_bitcast_fusion.8
  210.7 70.5 %all-reduce.1 = (f32[128,16]{0,1:T(8,128)}, f32[384]{0:T(512)}) all-reduce(f32[128,16]{0,1:T(8,128)S(1)} %copy-done.49, f32[384]{0:T(512)S(1)} %reshape.177), channel_id=1, replica_groups=mesh['dap'=16,'dp'=8] {'dap','dp'}, use_global_device_ids=true, to_apply=%region_31.32 | all-reduce | flops 2432 | bytes 19456 | tf_op jit(solution)/shard_map/psum | solution.py:150
  283.6 100.0 %all-reduce.8.cloned.1.call-done = (f32[128,512]{1,0:T(8,128)}, f32[128,512]{1,0:T(8,128)}, f32[512,128]{1,0:T(8,128)}, f32[384,384]{1,0:T(8,128)}, f32[384,768]...) async-done(((f32[128,512]{1,0:T(8,128)}, f32[128,512]{1,0:T(8,128)}, ...) | async-done | bytes 10813456 | tf_op jit(solution)/shard_map/psum | solution.py:150
  388.7 2.0 copy.211
  (353 shorter events, 136.8 us)
Async XLA Ops:
  7.2 84.0 %copy-start = (bf16[1536,384]{1,0:T(8,128)(2,1)S(1)}, bf16[1536,384]{1,0:T(8,128)(2,1)}, u32[]{:S(2)}) copy-start(bf16[1536,384]{1,0:T(8,128)(2,1)} %param.37) | copy-start | bytes 3538948
  7.2 200.5 %all-reduce.6.cloned.1.call-start = ((), (), s32[]{:S(2)}) async-start(), calls=%async_computation | async-start | bytes 1572864
  10.1 76.3 %copy-start.41 = (f32[4,8]{1,0:T(4,128)}, f32[4,8]{1,0:T(4,128)S(1)}, u32[]{:S(2)}) copy-start(f32[4,8]{1,0:T(4,128)S(1)} %broadcast_multiply_fusion.13) | copy-start | bytes 388
  11.0 75.4 %copy-start.43 = (f32[4,8]{1,0:T(4,128)}, f32[4,8]{1,0:T(4,128)S(1)}, u32[]{:S(2)}) copy-start(f32[4,8]{1,0:T(4,128)S(1)} %add_rsqrt_fusion.5) | copy-start | bytes 388
  38.7 4.5 %copy-start.1 = (bf16[128,512]{1,0:T(8,128)(2,1)S(1)}, bf16[128,512]{1,0:T(8,128)(2,1)}, u32[]{:S(2)}) copy-start(bf16[128,512]{1,0:T(8,128)(2,1)} %param.27) | copy-start | bytes 393220
  38.7 4.5 %copy-start.2 = (bf16[128,512]{1,0:T(8,128)(2,1)S(1)}, bf16[128,512]{1,0:T(8,128)(2,1)}, u32[]{:S(2)}) copy-start(bf16[128,512]{1,0:T(8,128)(2,1)} %param.26) | copy-start | bytes 393220
  86.4 4.5 %copy-start.7 = (bf16[384,1536]{1,0:T(8,128)(2,1)S(1)}, bf16[384,1536]{1,0:T(8,128)(2,1)}, u32[]{:S(2)}) copy-start(bf16[384,1536]{1,0:T(8,128)(2,1)} %param.36) | copy-start | bytes 3538948
  86.4 4.8 %copy-start.46 = (bf16[4,8,384]{2,1,0:T(8,128)(2,1)S(1)}, bf16[4,8,384]{2,1,0:T(8,128)(2,1)}, u32[]{:S(2)}) copy-start(bf16[4,8,384]{2,1,0:T(8,128)(2,1)} %param.25) | copy-start | bytes 73732
  87.7 3.2 copy-start.37
  89.2 2.6 copy-start.8
  104.3 9.0 %copy-start.48 = (f32[4,128]{1,0:T(4,128)S(1)}, f32[4,128]{1,0:T(4,128)}, u32[]{:S(2)}) copy-start(f32[4,128]{1,0:T(4,128)} %add_multiply_fusion) | copy-start | bytes 6148
  110.4 273.1 %all-reduce.8.cloned.1.call-start = ((), (), s32[]{:S(2)}) async-start(), calls=%async_computation.1 | async-start | bytes 21626880 | tf_op jit(solution)/shard_map/psum | solution.py:150
  143.7 2.5 copy-start.34
  163.8 2.5 copy-start.34
  194.4 5.0 %copy-start.50 = (u32[128]{0:T(128)S(1)}, u32[128]{0:T(128)}, u32[]{:S(2)}) copy-start(u32[128]{0:T(128)} %constant.98) | copy-start | bytes 1540
  194.4 6.3 %copy-start.15 = (bf16[4,8,384]{2,1,0:T(8,128)(2,1)S(1)}, bf16[4,8,384]{2,1,0:T(8,128)(2,1)}, u32[]{:S(2)}) copy-start(bf16[4,8,384]{2,1,0:T(8,128)(2,1)} %param.22) | copy-start | bytes 73732
  194.4 6.3 %copy-start.38 = (bf16[4,8,384]{2,1,0:T(8,128)(2,1)S(1)}, bf16[4,8,384]{2,1,0:T(8,128)(2,1)}, u32[]{:S(2)}) copy-start(bf16[4,8,384]{2,1,0:T(8,128)(2,1)} %get-tuple-element.373) | copy-start | bytes 73732
  194.4 6.3 %copy-start.42 = (f32[4,8]{1,0:T(4,128)S(1)}, f32[4,8]{1,0:T(4,128)}, u32[]{:S(2)}) copy-start(f32[4,8]{1,0:T(4,128)} %copy-done.41) | copy-start | bytes 388
  194.4 6.3 %copy-start.44 = (f32[4,8]{1,0:T(4,128)S(1)}, f32[4,8]{1,0:T(4,128)}, u32[]{:S(2)}) copy-start(f32[4,8]{1,0:T(4,128)} %copy-done.43) | copy-start | bytes 388
  194.4 7.5 %copy-start.29 = (bf16[4,8,384]{2,1,0:T(8,128)(2,1)S(1)}, bf16[4,8,384]{2,1,0:T(8,128)(2,1)}, u32[]{:S(2)}) copy-start(bf16[4,8,384]{2,1,0:T(8,128)(2,1)} %copy-done.28) | copy-start | bytes 73732
  194.4 7.5 %copy-start.36 = (bf16[4,8,1536]{2,1,0:T(8,128)(2,1)S(1)}, bf16[4,8,1536]{2,1,0:T(8,128)(2,1)}, u32[]{:S(2)}) copy-start(bf16[4,8,1536]{2,1,0:T(8,128)(2,1)} %copy-done.35) | copy-start | bytes 294916
  200.7 3.1 copy-start.40
  209.9 71.3 %copy-start.17 = (bf16[384,384]{1,0:T(8,128)(2,1)S(1)}, bf16[384,384]{1,0:T(8,128)(2,1)}, u32[]{:S(2)}) copy-start(bf16[384,384]{1,0:T(8,128)(2,1)} %param.33) | copy-start | bytes 884740
  209.9 71.5 %copy-start.27 = (bf16[384,384]{1,0:T(8,128)(2,1)S(1)}, bf16[384,384]{1,0:T(8,128)(2,1)}, u32[]{:S(2)}) copy-start(bf16[384,384]{1,0:T(8,128)(2,1)} %param.30) | copy-start | bytes 884740
  209.9 71.7 %copy-start.14 = (bf16[384,768]{1,0:T(8,128)(2,1)S(1)}, bf16[384,768]{1,0:T(8,128)(2,1)}, u32[]{:S(2)}) copy-start(bf16[384,768]{1,0:T(8,128)(2,1)} %param.32) | copy-start | bytes 1769476
  209.9 72.9 %copy-start.25 = (f32[4,8,384]{2,1,0:T(8,128)S(1)}, f32[4,8,384]{2,1,0:T(8,128)}, u32[]{:S(2)}) copy-start(f32[4,8,384]{2,1,0:T(8,128)} %copy-done.24) | copy-start | bytes 147460
  383.6 7.2 %copy-start.16 = (f32[384,768]{1,0:T(8,128)S(1)}, f32[384,768]{1,0:T(8,128)}, u32[]{:S(2)}) copy-start(f32[384,768]{1,0:T(8,128)} %get-tuple-element.628) | copy-start | bytes 3538948
  387.0 4.7 %copy-start.21 = (f32[384,384]{1,0:T(8,128)S(1)}, f32[384,384]{1,0:T(8,128)}, u32[]{:S(2)}) copy-start(f32[384,384]{1,0:T(8,128)} %get-tuple-element.629) | copy-start | bytes 1769476
  388.7 3.8 copy-start.20
  390.7 2.7 copy-start.13
  393.4 2.5 copy-start.12
  395.9 2.5 copy-start.11
  (39 other events, 47.1 us)
Sparse Core Ops, SparseCore 0:
  110.6 88.9 all-reduce.5
  210.1 173.4 all-reduce.7
where the time goes:
time: 410 us; the launch traced here: 407 us
  waiting for transfers between devices  100 us (24%)
  matrix products  95.2 us (23%)
  blocking collectives  92.2 us (22%)
  local copies, waits for them, and re-layouts  74.5 us (18%)
  other arithmetic  28.4 us (7%)
  between operations  15.2 us (4%)
    psum x1, waiting for transfers between devices, body(): lax.psum(pair_grads + (d_w_q, d_q_bias, d_w_kv, d_w_g, d_w_o, d_w_sa, d_w...  100 us
    dot_general x78, matrix products, contract(): jnp.einsum(equation, left_op, right_op, preferred_element_type=jnp.float32)  95.2 us
    psum x1, blocking collectives, body(): lax.psum(pair_grads + (d_w_q, d_q_bias, d_w_kv, d_w_g, d_w_o, d_w_sa, d_w...  70.5 us
    all_gather x1, blocking collectives, body(): kv_all = lax.all_gather(kv_local, 'dap', axis=1, tiled=True)  21.7 us
    unnamed x102, local copies, waits for them, and re-layouts  20.3 us
    dynamic_update_slice x12, local copies, waits for them, and re-layouts, body(): z_new, bias_rows = lax.map(forward_rows, z_blocks)  16.4 us
    dynamic_slice x8, local copies, waits for them, and re-layouts, body(): z_new, bias_rows = lax.map(forward_rows, z_blocks)  13.8 us
  transfers between devices with their start and end apart: 2, of which 1 were waited for; matrix products, arithmetic and copies ran while one was open for 23% of the time, Pallas kernels for 0%

commit v1 on v0

v1 whole, which is shorter than its diff:
```python
import functools

import jax
import jax.numpy as jnp
from jax import lax
from jax.experimental import pallas as pl
from jax.experimental.pallas import tpu as pltpu
from jax.sharding import PartitionSpec as P

HEAD_DIM = 24
EPSILON = 1e-5
MASK_BIG = 1e9
BLOCK = 512
F32 = jnp.float32
BF16 = jnp.bfloat16


def mm(lhs, rhs):
    return lax.dot_general(lhs, rhs, (((1,), (0,)), ((), ())), preferred_element_type=F32)


def mm_nt(lhs, rhs):
    return lax.dot_general(lhs, rhs, (((1,), (1,)), ((), ())), preferred_element_type=F32)


def mm_tn(lhs, rhs):
    return lax.dot_general(lhs, rhs, (((0,), (0,)), ((), ())), preferred_element_type=F32)


def layer_norm(values):
    wide_vals = values.astype(F32)
    centred = wide_vals - jnp.mean(wide_vals, axis=-1, keepdims=True)
    inv_std = lax.rsqrt(jnp.mean(centred * centred, axis=-1, keepdims=True) + EPSILON)
    return centred * inv_std, inv_std


def norm_grad(normed, inv_std, grad_out):
    mean_grad = jnp.mean(grad_out, axis=-1, keepdims=True)
    mean_proj = jnp.mean(grad_out * normed, axis=-1, keepdims=True)
    return inv_std * (grad_out - mean_grad - normed * mean_proj)


def sigmoid(values):
    return 0.5 + 0.5 * jnp.tanh(0.5 * values)


def swiglu(hid_a, hid_b):
    half = 0.5 * hid_a
    return half * (1.0 + jnp.tanh(half)) * hid_b


def swiglu_and_grad(hid_a, hid_b, grad_hidden):
    half = 0.5 * hid_a
    plus = 1.0 + jnp.tanh(half)
    silu = half * plus
    sig = 0.5 * plus
    grad_b = grad_hidden * silu
    grad_a = grad_hidden * hid_b * (sig + silu * (1.0 - sig))
    return silu * hid_b, grad_a, grad_b


def pair_forward_kernel(z_ref, w_ab_ref, w_po_ref, w_bias_t_ref, z_new_ref, bias_ref):
    width = w_po_ref.shape[0]
    z_rows = z_ref[...]
    normed, _ = layer_norm(z_rows)
    hid = mm(normed.astype(BF16), w_ab_ref[...])
    hidden = swiglu(hid[:, :width], hid[:, width:]).astype(BF16)
    z_new = (z_rows.astype(F32) + mm(hidden, w_po_ref[...])).astype(BF16)
    z_new_ref[...] = z_new
    bias_norm, _ = layer_norm(z_new)
    bias = mm_nt(w_bias_t_ref[...], bias_norm.astype(BF16))
    heads = w_bias_t_ref.shape[0]
    tok = bias_ref.shape[1]
    for row in range(bias.shape[1] // tok):
        bias_ref[row * heads:(row + 1) * heads, :] = bias[:, row * tok:(row + 1) * tok]


def pair_forward(z_rows, w_ab, w_po, w_bias_t, tok):
    rows, chan = z_rows.shape
    heads = w_bias_t.shape[0]
    width = w_po.shape[0]
    whole = lambda shape: pl.BlockSpec(shape, lambda i: (0, 0))
    return pl.pallas_call(
        pair_forward_kernel,
        grid=(rows // BLOCK,),
        in_specs=[pl.BlockSpec((BLOCK, chan), lambda i: (i, 0)), whole((chan, 2 * width)), whole((width, chan)), whole((heads, chan))],
        out_specs=[pl.BlockSpec((BLOCK, chan), lambda i: (i, 0)), pl.BlockSpec((BLOCK // tok * heads, tok), lambda i: (i, 0))],
        out_shape=[jax.ShapeDtypeStruct((rows, chan), BF16), jax.ShapeDtypeStruct((rows // tok * heads, tok), F32)],
        name="pair_forward",
        cost_estimate=pl.CostEstimate(flops=6 * rows * chan * width, bytes_accessed=4 * rows * chan, transcendentals=0),
    )(z_rows, w_ab, w_po, w_bias_t)


def pair_backward_kernel(z_ref, zn_ref, dz_ref, gl_ref, w_ab_ref, w_ab_t_ref, w_po_t_ref, w_bias_t_ref, dzi_ref, dwab_ref, dwpo_t_ref, dwb_t_ref):
    width = w_po_t_ref.shape[1]
    heads = w_bias_t_ref.shape[0]

    @pl.when(pl.program_id(0) == 0)
    def _():
        dwab_ref[...] = jnp.zeros_like(dwab_ref)
        dwpo_t_ref[...] = jnp.zeros_like(dwpo_t_ref)
        dwb_t_ref[...] = jnp.zeros_like(dwb_t_ref)

    bias_norm, bias_inv = layer_norm(zn_ref[...])
    groups = gl_ref.shape[0] // heads
    gl = jnp.concatenate([gl_ref[k * heads:(k + 1) * heads, :] for k in range(groups)], axis=1)
    dwb_t_ref[...] += mm(gl, bias_norm.astype(BF16))
    grad_norm = mm_tn(gl, w_bias_t_ref[...])
    grad_new = dz_ref[...].astype(F32) + norm_grad(bias_norm, bias_inv, grad_norm)
    grad_new_bf = grad_new.astype(BF16)
    normed, inv_std = layer_norm(z_ref[...])
    normed_bf = normed.astype(BF16)
    hid = mm(normed_bf, w_ab_ref[...])
    grad_hidden = mm(grad_new_bf, w_po_t_ref[...])
    hidden, grad_a, grad_b = swiglu_and_grad(hid[:, :width], hid[:, width:], grad_hidden)
    dwpo_t_ref[...] += mm_tn(grad_new_bf, hidden.astype(BF16))
    grad_ab = jnp.concatenate([grad_a.astype(BF16), grad_b.astype(BF16)], axis=1)
    dwab_ref[...] += mm_tn(normed_bf, grad_ab)
    grad_normed = mm(grad_ab, w_ab_t_ref[...])
    dzi_ref[...] = (grad_new + norm_grad(normed, inv_std, grad_normed)).astype(BF16)


def pair_backward(z_rows, z_new, dz_rows, grad_logits, w_ab, w_ab_t, w_po_t, w_bias_t, tok):
    rows, chan = z_rows.shape
    heads = w_bias_t.shape[0]
    width = w_po_t.shape[1]
    whole = lambda shape: pl.BlockSpec(shape, lambda i: (0, 0))
    row_spec = pl.BlockSpec((BLOCK, chan), lambda i: (i, 0))
    return pl.pallas_call(
        pair_backward_kernel,
        grid=(rows // BLOCK,),
        in_specs=[row_spec, row_spec, row_spec, pl.BlockSpec((BLOCK // tok * heads, tok), lambda i: (i, 0)), whole((chan, 2 * width)), whole((2 * width, chan)), whole((chan, width)), whole((heads, chan))],
        out_specs=[row_spec, whole((chan, 2 * width)), whole((chan, width)), whole((heads, chan))],
        out_shape=[jax.ShapeDtypeStruct((rows, chan), BF16), jax.ShapeDtypeStruct((chan, 2 * width), F32), jax.ShapeDtypeStruct((chan, width), F32), jax.ShapeDtypeStruct((heads, chan), F32)],
        name="pair_backward",
        cost_estimate=pl.CostEstimate(flops=16 * rows * chan * width, bytes_accessed=8 * rows * chan, transcendentals=0),
    )(z_rows, z_new, dz_rows, grad_logits, w_ab, w_ab_t, w_po_t, w_bias_t)


def single_kernel(tok, s_all_ref, s_ref, ds_ref, mask_ref, bias_ref, w_q_ref, q_bias_ref, w_kv_ref, w_g_ref, w_o_ref, w_sa_ref, w_sb_ref, w_so_ref,
                  gl_ref, part_ref, gact_ref, gmid_ref, dwq_ref, dqb_ref, dwkv_ref, dwg_ref, dwo_ref, dwsa_ref, dwsb_ref, dwso_ref,
                  q_exp, g_exp, prob, gkv):
    rows, chan = s_ref.shape
    num_cplx = s_all_ref.shape[0] // tok
    heads = bias_ref.shape[0] // rows
    per = rows // num_cplx * heads
    scale = HEAD_DIM ** -0.5
    flat = rows * heads

    def expand(values):
        pick = lax.broadcasted_iota(jnp.int32, (flat, rows), 0) // heads == lax.broadcasted_iota(jnp.int32, (flat, rows), 1)
        return mm(pick.astype(BF16), values)

    def head_mask(count):
        head = lax.broadcasted_iota(jnp.int32, (count, chan), 0) % heads
        col = lax.broadcasted_iota(jnp.int32, (count, chan), 1)
        return (col >= head * HEAD_DIM) & (col < head * HEAD_DIM + HEAD_DIM)

    def fold(values):
        kept = jnp.where(head_mask(values.shape[0]), values, 0.0)
        return jnp.sum(kept.reshape(values.shape[0] // heads, heads, chan), axis=1)

    a_all, _ = layer_norm(s_all_ref[...])
    a_all = a_all.astype(BF16)
    kv = mm(a_all, w_kv_ref[...]).astype(BF16)
    s_wide = s_ref[...].astype(F32)
    s_norm, _ = layer_norm(s_wide)
    act = s_norm.astype(BF16)
    queries = (mm(act, w_q_ref[...]) + q_bias_ref[...].astype(F32)).astype(BF16)
    gate = sigmoid(mm(act, w_g_ref[...]))
    q_exp[...] = jnp.where(head_mask(flat), expand(queries), 0.0).astype(BF16)
    key_mask = MASK_BIG * (mask_ref[...].astype(F32) - 1.0)
    attended = []
    for b in range(num_cplx):
        keys = kv[b * tok:(b + 1) * tok, :chan]
        vals = kv[b * tok:(b + 1) * tok, chan:]
        logits = mm_nt(q_exp[b * per:(b + 1) * per, :], keys) * scale + bias_ref[b * per:(b + 1) * per, :] + key_mask[b:b + 1, :]
        weight = jnp.exp(logits - jnp.max(logits, axis=-1, keepdims=True))
        p_wide = weight / jnp.sum(weight, axis=-1, keepdims=True)
        prob[b * per:(b + 1) * per, :] = p_wide
        attended.append(fold(mm(p_wide.astype(BF16), vals)))
    attended = jnp.concatenate(attended, axis=0)
    gated = (gate * attended).astype(BF16)
    s_mid = (s_wide + mm(gated, w_o_ref[...])).astype(BF16)
    mid_norm, mid_inv = layer_norm(s_mid)
    mid_act = mid_norm.astype(BF16)
    trans_a = mm(mid_act, w_sa_ref[...])
    trans_b = mm(mid_act, w_sb_ref[...])
    ds_rows = ds_ref[...]
    grad_hidden = mm_nt(ds_rows, w_so_ref[...])
    hidden, grad_ta, grad_tb = swiglu_and_grad(trans_a, trans_b, grad_hidden)
    grad_ta = grad_ta.astype(BF16)
    grad_tb = grad_tb.astype(BF16)
    dwso_ref[...] = mm_tn(hidden.astype(BF16), ds_rows)
    dwsa_ref[...] = mm_tn(mid_act, grad_ta)
    dwsb_ref[...] = mm_tn(mid_act, grad_tb)
    grad_mid_norm = mm_nt(grad_ta, w_sa_ref[...]) + mm_nt(grad_tb, w_sb_ref[...])
    grad_mid = ds_rows.astype(F32) + norm_grad(mid_norm, mid_inv, grad_mid_norm)
    grad_mid_bf = grad_mid.astype(BF16)
    gmid_ref[...] = grad_mid
    dwo_ref[...] = mm_tn(gated, grad_mid_bf)
    grad_gated = mm_nt(grad_mid_bf, w_o_ref[...])
    grad_gate = (grad_gated * attended * gate * (1.0 - gate)).astype(BF16)
    grad_att = (grad_gated * gate).astype(BF16)
    g_exp[...] = jnp.where(head_mask(flat), expand(grad_att), 0.0).astype(BF16)
    grad_query = []
    for b in range(num_cplx):
        keys = kv[b * tok:(b + 1) * tok, :chan]
        vals = kv[b * tok:(b + 1) * tok, chan:]
        p_wide = prob[b * per:(b + 1) * per, :]
        g_rows = g_exp[b * per:(b + 1) * per, :]
        grad_prob = mm_nt(g_rows, vals)
        grad_logits = (p_wide * (grad_prob - jnp.sum(p_wide * grad_prob, axis=-1, keepdims=True))).astype(BF16)
        gl_ref[b * per:(b + 1) * per, :] = grad_logits
        grad_query.append(fold(mm(grad_logits, keys)) * scale)
        gkv[b * tok:(b + 1) * tok, :chan] = (mm_tn(grad_logits, q_exp[b * per:(b + 1) * per, :]) * scale).astype(BF16)
        gkv[b * tok:(b + 1) * tok, chan:] = mm_tn(p_wide.astype(BF16), g_rows).astype(BF16)
    grad_query = jnp.concatenate(grad_query, axis=0)
    grad_query_bf = grad_query.astype(BF16)
    dwkv_ref[...] = mm_tn(a_all, gkv[...])
    part_ref[...] = mm_nt(gkv[...], w_kv_ref[...]).astype(BF16)
    dwq_ref[...] = mm_tn(act, grad_query_bf)
    dqb_ref[...] = jnp.sum(grad_query, axis=0, keepdims=True)
    dwg_ref[...] = mm_tn(act, grad_gate)
    gact_ref[...] = mm_nt(grad_query_bf, w_q_ref[...]) + mm_nt(grad_gate, w_g_ref[...])


def single_track(tok, s_all, s_rows, ds_rows, mask, bias, weights):
    rows, chan = s_rows.shape
    flat = bias.shape[0]
    all_rows = s_all.shape[0]
    shapes = [((flat, tok), BF16), ((all_rows, chan), BF16), ((rows, chan), F32), ((rows, chan), F32)] + [(w.shape, F32) for w in weights]
    return pl.pallas_call(
        functools.partial(single_kernel, tok),
        out_shape=[jax.ShapeDtypeStruct(*s) for s in shapes],
        in_specs=[pl.BlockSpec(memory_space=pltpu.VMEM)] * (5 + len(weights)),
        out_specs=[pl.BlockSpec(memory_space=pltpu.VMEM)] * len(shapes),
        scratch_shapes=[pltpu.VMEM((flat, chan), BF16), pltpu.VMEM((flat, chan), BF16), pltpu.VMEM((flat, tok), F32), pltpu.VMEM((all_rows, 2 * chan), BF16)],
        name="single_track",
        cost_estimate=pl.CostEstimate(flops=3 * 10**9, bytes_accessed=20 * 2**20, transcendentals=0),
    )(s_all, s_rows, ds_rows, mask, bias, *weights)


def solution(mesh):
    pair_spec = P('dp', 'dap', None, None)
    single_spec = P('dp', 'dap', None)

    def body(pair_z, single_s, token_mask, dz_out, ds_out, w_pa, w_pb, w_po, w_bias, w_q, q_bias, w_kv, w_g, w_o, w_sa, w_sb, w_so):
        num_cplx, num_rows, tok, pair_dim = pair_z.shape
        chan = single_s.shape[-1]
        width = w_pa.shape[1]
        w_ab = jnp.concatenate([w_pa, w_pb], axis=1)
        w_ab_t = w_ab.T
        w_bias_t = w_bias.T
        z_rows = pair_z.reshape(-1, pair_dim)
        dz_rows = dz_out.reshape(-1, pair_dim)
        s_all = lax.all_gather(single_s, 'dap', axis=1, tiled=True).reshape(-1, chan)
        z_new, bias = pair_forward(z_rows, w_ab, w_po, w_bias_t, tok)
        s_rows = single_s.reshape(-1, chan)
        outs = single_track(tok, s_all, s_rows, ds_out.reshape(-1, chan), token_mask, bias, (w_q, q_bias[None], w_kv, w_g, w_o, w_sa, w_sb, w_so))
        grad_logits, part, gact, gmid = outs[:4]
        dwq, dqb, dwkv, dwg, dwo, dwsa, dwsb, dwso = outs[4:]
        part_sum = lax.psum_scatter(part.reshape(num_cplx, -1, chan), 'dap', scatter_dimension=1, tiled=True)
        s_norm, s_inv = layer_norm(s_rows)
        ds_in = (gmid + norm_grad(s_norm, s_inv, gact + part_sum.reshape(-1, chan).astype(F32))).astype(BF16)
        dz_in, dwab, dwpo_t, dwb_t = pair_backward(z_rows, z_new, dz_rows, grad_logits, w_ab, w_ab_t, w_po.T, w_bias_t, tok)
        grads = (dwab[:, :width], dwab[:, width:], dwpo_t.T, dwb_t.T, dwq, dqb[0], dwkv, dwg, dwo, dwsa, dwsb, dwso)
        grads = lax.psum(grads, ('dap', 'dp'))
        return (dz_in.reshape(pair_z.shape), ds_in.reshape(single_s.shape)) + tuple(grads)

    in_specs = (pair_spec, single_spec, P('dp', None), pair_spec, single_spec) + (P(),) * 12
    out_specs = (pair_spec, single_spec) + (P(),) * 12
    return jax.shard_map(body, mesh=mesh, in_specs=in_specs, out_specs=out_specs, check_vma=False)
```

time: 410 us -> 349 us (0.85)
  matrix products: 95.2 us -> 0 us
  waiting for transfers between devices: 100 us -> 169 us
  local copies, waits for them, and re-layouts: 74.5 us -> 24.6 us
  Pallas kernels: 0 us -> 44.3 us
  other arithmetic: 28.4 us -> 3.4 us
    dot_general x78 -> x0, matrix products: 95.2 us -> none  [contract(): jnp.einsum(equation, left_op, right_op, preferred_element_type=jnp.float32)]
    psum x1, waiting for transfers between devices: 100 us -> 169 us  [body(): grads = lax.psum(grads, ('dap', 'dp'))]
    pallas_call x0 -> x3, Pallas kernels: none -> 44.3 us  [the longest x1 18.2 us: pair_backward(): pl.pallas_call(pair_backward_kernel, grid=(rows // BLOCK,), in_specs=[row...]
    dynamic_slice x12 -> x0, local copies, waits for them, and re-layouts: 16.9 us -> none  [the longest x8 13.8 us: body(): z_new, bias_rows = lax.map(forward_rows, z_blocks)]
    dynamic_update_slice x12 -> x0, local copies, waits for them, and re-layouts: 16.4 us -> none  [body(): z_new, bias_rows = lax.map(forward_rows, z_blocks)]
    reshape x6 -> x0, local copies, waits for them, and re-layouts: 8.07 us -> none  [the longest x1 1.91 us: body(): grad_values.reshape(num_cplx, num_tok, attn_width)]
    while x49 -> x0, local copies, waits for them, and re-layouts: 7.13 us -> none
    reduce_sum x18 -> x1, other arithmetic: 6.21 us -> 0.16 us  [layer_norm(): jnp.mean(centred * centred, axis=-1, keepdims=True) + EPSILON]
  transfers between devices with their start and end apart: 2 -> 2, of which waited for: 1 -> 1; matrix products, arithmetic and copies ran while one was open for 23% -> 2% of each run, Pallas kernels for 0% -> 5%
where the time goes in v1:
time: 349 us; the launch traced here: 348 us
  waiting for transfers between devices  169 us (48%)
  blocking collectives  91.5 us (26%)
  Pallas kernels  44.3 us (13%)
  local copies, waits for them, and re-layouts  24.6 us (7%)
  between operations  14.8 us (4%)
    psum x1, waiting for transfers between devices, body(): grads = lax.psum(grads, ('dap', 'dp'))  169 us
    psum x1, blocking collectives, body(): grads = lax.psum(grads, ('dap', 'dp'))  69.2 us
    all_gather x1, blocking collectives, body(): lax.all_gather(single_s, 'dap', axis=1, tiled=True).reshape(-1, chan)  22.3 us
    unnamed x40, local copies, waits for them, and re-layouts  20.4 us
    pallas_call x1, Pallas kernels, pair_backward(): pl.pallas_call(pair_backward_kernel, grid=(rows // BLOCK,), in_specs=[row...  18.2 us
    pallas_call x1, Pallas kernels, single_track(): pl.pallas_call(functools.partial(single_kernel, tok), out_shape=[jax.Shap...  14.9 us
    pallas_call x1, Pallas kernels, pair_forward(): pl.pallas_call(pair_forward_kernel, grid=(rows // BLOCK,), in_specs=[pl.B...  11.2 us
  transfers between devices with their start and end apart: 2, of which 1 were waited for; matrix products, arithmetic and copies ran while one was open for 2% of the time, Pallas kernels for 5%

profile of v1, /device:TPU:1, one launch (start us, length us, event | category | flops | bytes accessed | tf_op | source)
XLA Modules:
  0.0 347.9 jit_solution(6033524029339393886)
XLA Ops:
  7.2 1.0 copy.38
  8.3 1.0 copy.37
  9.3 0.7 fusion.4
  10.0 0.8 copy.39.w_ab_ref
  10.9 22.3 %all_gather.3 = bf16[4,128,384]{2,1,0:T(8,128)(2,1)} all-gather(bf16[4,8,384]{2,1,0:T(8,128)(2,1)} %param.18), channel_id=1, replica_groups=mesh['dap'=16,'dp'=8] {'dap'}, dimensions={1}, use_global_device_ids=true | all-gather | bytes 417792 | tf_op jit(solution)/shard_map/all_gather | solution.py:257
  33.2 1.2 broadcast_in_dim.2.q_bias_ref
  34.4 11.2 %pair_forward.1 = (bf16[4096,128]{1,0:T(8,128)(2,1)}, f32[512,128]{1,0:T(8,128)}) custom-call(bf16[4096,128]{1,0:T(8,128)(2,1)} %bitcast.35, bf16[128,1024]{1,0:T(8,128)(2,1)} %copy.39.w_ab_ref, bf16[512,128]{1,0:T(8,128)(2,1)} %w_po_ref.1, bf16[16,128]{1,0:T(8,128)(2,1)} %bitcast.39), custom_call_target="tpu_custom_call" | custom-call | flops 1610612736 | bytes 2097152 | tf_op jit(solution)/shard_map/pair_forward/pallas_call | solution.py:83
  45.7 14.9 %single_track.1 = (bf16[512,128]{1,0:T(8,128)(2,1)}, bf16[512,384]{1,0:T(8,128)(2,1)}, f32[32,384]{1,0:T(8,128)}, f32[32,384]{1,0:T(8,128)}, f32[384,384]{1,0:T(...) custom-call(bf16[512,384]{1,0:T(8,128)(2,1)} %bitcast.31, ...), custom_call_target="tpu_custom_call" | custom-call | flops 3000000000 | bytes 20971520 | tf_op jit(solution)/shard_map/single_track/pallas_call | solution.py:233
  60.6 0.8 copy.40
  61.4 18.2 %pair_backward.1 = (bf16[4096,128]{1,0:T(8,128)(2,1)}, f32[128,1024]{1,0:T(8,128)}, f32[128,512]{1,0:T(8,128)}, f32[16,128]{1,0:T(8,128)}) custom-call(bf16[4096,128]{1,0:T(8,128)(2,1)} %bitcast.36, bf16[4096,128]{1,0:T(8,128)(2,1)} %get-tuple-element.32.zn_ref, bf16[4096,128]{1,0:T(8,128)(2,1)} %bitcast.37, bf16[512,128]{1,0:T(8,128)(2,1)} %get-tuple-element.34.gl_ref, ...), custom_call_target="tpu_custom_call" | custom-call | flops 4294967296 | bytes 4194304 | tf_op jit(solution)/shard_map/pair_backward/pallas_call | solution.py:129
  79.6 1.9 fusion.5
  81.5 0.7 copy-done.4
  82.2 0.1 convert_reduce_fusion
  82.4 0.2 fusion.1
  82.5 0.1 rsqrt.12
  82.6 0.6 dynamic-slice
  83.9 69.2 %all-reduce.1 = (f32[128,16]{0,1:T(8,128)}, f32[384]{0:T(512)}) all-reduce(f32[128,16]{0,1:T(8,128)S(1)} %bitcast.34, f32[384]{0:T(512)S(1)} %reduce.2), channel_id=1, replica_groups=mesh['dap'=16,'dp'=8] {'dap','dp'}, use_global_device_ids=true, to_apply=%region_8.0 | all-reduce | flops 2432 | bytes 19456 | tf_op jit(solution)/shard_map/psum | solution.py:268
  153.1 0.9 fusion.3
  154.0 1.4 fusion.2
  155.4 169.2 %all-reduce.8.cloned.1.call-done = (f32[128,512]{1,0:T(8,128)}, f32[128,512]{1,0:T(8,128)}, f32[512,128]{0,1:T(8,128)}, f32[384,384]{1,0:T(8,128)}, f32[384,768]...) async-done(((f32[128,512]{1,0:T(8,128)}, f32[128,512]{1,0:T(8,128)}, ...) | async-done | bytes 10813456 | tf_op jit(solution)/shard_map/psum | solution.py:268
  324.7 1.9 copy.42
  326.5 1.7 copy.56
  328.3 1.7 copy.57
  329.9 2.0 copy.58
  331.9 1.0 copy.59
  332.9 0.8 copy.60
  333.8 0.8 copy.61
  334.6 1.4 copy.62
  336.0 1.1 copy-done.1
  337.1 1.4 copy.63
  338.5 1.1 copy-done
  339.6 1.4 copy.64
  (33 shorter events, 0.3 us)
Async XLA Ops:
  7.2 145.9 %all-reduce.6.cloned.1.call-start = ((), (), s32[]{:S(2)}) async-start(), calls=%async_computation | async-start | bytes 786432
  45.7 15.0 %copy-start.8 = (bf16[512,128]{1,0:T(8,128)(2,1)S(1)}, bf16[512,128]{1,0:T(8,128)(2,1)}, u32[]{:S(2)}) copy-start(bf16[512,128]{1,0:T(8,128)(2,1)} %w_po_ref.1) | copy-start | bytes 393220
  60.6 264.1 %all-reduce.8.cloned.1.call-start = ((), (), s32[]{:S(2)}) async-start(), calls=%async_computation.1 | async-start | bytes 21626880 | tf_op jit(solution)/shard_map/psum | solution.py:268
  81.4 0.7 copy-start.4
  81.4 1.2 copy-start.12
  81.4 2.4 copy-start.11
  81.4 2.4 copy-start.10
  81.4 71.6 %copy-start.7 = (f32[32,384]{1,0:T(8,128)S(1)}, f32[32,384]{1,0:T(8,128)}, u32[]{:S(2)}) copy-start(f32[32,384]{1,0:T(8,128)} %get-tuple-element.37) | copy-start | bytes 147460
  81.5 72.5 %copy-start.9 = (f32[32,384]{1,0:T(8,128)S(1)}, f32[32,384]{1,0:T(8,128)}, u32[]{:S(2)}) copy-start(f32[32,384]{1,0:T(8,128)} %get-tuple-element.36) | copy-start | bytes 147460
  324.7 7.3 %copy-start.3 = (f32[384,768]{1,0:T(8,128)S(1)}, f32[384,768]{1,0:T(8,128)}, u32[]{:S(2)}) copy-start(f32[384,768]{1,0:T(8,128)} %get-tuple-element.106) | copy-start | bytes 3538948
  326.5 6.4 %copy-start.6 = (f32[384,384]{1,0:T(8,128)S(1)}, f32[384,384]{1,0:T(8,128)}, u32[]{:S(2)}) copy-start(f32[384,384]{1,0:T(8,128)} %get-tuple-element.107) | copy-start | bytes 1769476
  329.9 3.8 %copy-start.5 = (f32[384,384]{1,0:T(8,128)S(1)}, f32[384,384]{1,0:T(8,128)}, u32[]{:S(2)}) copy-start(f32[384,384]{1,0:T(8,128)} %get-tuple-element.108) | copy-start | bytes 1769476
  331.9 2.7 copy-start.2
  334.6 2.5 copy-start.1
  337.1 2.5 copy-start
Sparse Core Ops, SparseCore 0:
  60.7 86.9 all-reduce.5
  155.2 169.3 all-reduce.7

commit v2 on v1

--- a/solution.py
+++ b/solution.py
@@ -11,6 +11,13 @@
 EPSILON = 1e-5
 MASK_BIG = 1e9
 BLOCK = 512
+SIDE = 4
+PLANE = 16
+LANES = 128
+SHARDS = 96
+PIECE_ROWS = (144, 64, 16)
+ROUTES = (('x', 'y', 'z'), ('y', 'z', 'x'), ('z', 'x', 'y'))
+MESH = pl.DeviceIdType.MESH
 F32 = jnp.float32
 BF16 = jnp.bfloat16
 
@@ -59,7 +66,55 @@
     return silu * hid_b, grad_a, grad_b
 
 
-def pair_forward_kernel(z_ref, w_ab_ref, w_po_ref, w_bias_t_ref, z_new_ref, bias_ref):
+def position():
+    dap = lax.axis_index('dap')
+    dp = lax.axis_index('dp')
+    return {'dap': dap, 'dp': dp, 'z': dap // SIDE, 'y': dap % SIDE, 'x': dp // 2, 'core': dp % 2}
+
+
+def neighbour(here, axis, step):
+    moved = (here[axis] + step) % SIDE
+    if axis == 'x':
+        return {'dap': here['dap'], 'dp': moved * 2 + here['core']}
+    if axis == 'y':
+        return {'dap': here['z'] * SIDE + moved, 'dp': here['dp']}
+    return {'dap': moved * SIDE + here['y'], 'dp': here['dp']}
+
+
+def plane_member(here, step):
+    return {'dap': (here['dap'] + step) % PLANE, 'dp': here['dp']}
+
+
+def partner(here):
+    return {'dap': here['dap'], 'dp': here['x'] * 2 + 1 - here['core']}
+
+
+def meet(devices):
+    barrier = pltpu.get_barrier_semaphore()
+    for device in devices:
+        pl.semaphore_signal(barrier, inc=1, device_id=device, device_id_type=MESH)
+    pl.semaphore_wait(barrier, len(devices))
+
+
+def send(src, dst, send_sem, recv_sem, device):
+    pltpu.make_async_remote_copy(src_ref=src, dst_ref=dst, send_sem=send_sem, recv_sem=recv_sem, device_id=device, device_id_type=MESH).start()
+
+
+def wait_bytes(like, sem):
+    pltpu.make_async_copy(like, like, sem).wait()
+
+
+def pair_forward_kernel(z_ref, w_ab_ref, w_po_ref, w_bias_t_ref, s_ref, z_new_ref, bias_ref, bias_norm_ref, s_all_ref, held, send_sem, recv_sem):
+    here = position()
+    step = pl.program_id(0)
+
+    @pl.when(step == 0)
+    def _():
+        meet([plane_member(here, k) for k in range(1, PLANE)])
+        for k in range(1, PLANE):
+            send(s_ref, held.at[here['dap']], send_sem, recv_sem, plane_member(here, k))
+        held[here['dap']] = s_ref[...]
+
     width = w_po_ref.shape[0]
     z_rows = z_ref[...]
     normed, _ = layer_norm(z_rows)
@@ -68,30 +123,42 @@
     z_new = (z_rows.astype(F32) + mm(hidden, w_po_ref[...])).astype(BF16)
     z_new_ref[...] = z_new
     bias_norm, _ = layer_norm(z_new)
-    bias = mm_nt(w_bias_t_ref[...], bias_norm.astype(BF16))
+    bias_norm = bias_norm.astype(BF16)
+    bias_norm_ref[...] = bias_norm
+    bias = mm_nt(w_bias_t_ref[...], bias_norm)
     heads = w_bias_t_ref.shape[0]
     tok = bias_ref.shape[1]
     for row in range(bias.shape[1] // tok):
         bias_ref[row * heads:(row + 1) * heads, :] = bias[:, row * tok:(row + 1) * tok]
 
-
-def pair_forward(z_rows, w_ab, w_po, w_bias_t, tok):
+    @pl.when(step == pl.num_programs(0) - 1)
+    def _():
+        others = held.at[pl.ds(0, PLANE - 1)]
+        wait_bytes(others, recv_sem)
+        wait_bytes(others, send_sem)
+        s_all_ref[...] = held[...]
+
+
+def pair_forward(z_rows, w_ab, w_po, w_bias_t, s_rows, tok):
     rows, chan = z_rows.shape
     heads = w_bias_t.shape[0]
     width = w_po.shape[0]
-    whole = lambda shape: pl.BlockSpec(shape, lambda i: (0, 0))
+    whole = lambda shape: pl.BlockSpec(shape, lambda i: (0,) * len(shape))
+    row_spec = pl.BlockSpec((BLOCK, chan), lambda i: (i, 0))
     return pl.pallas_call(
         pair_forward_kernel,
         grid=(rows // BLOCK,),
-        in_specs=[pl.BlockSpec((BLOCK, chan), lambda i: (i, 0)), whole((chan, 2 * width)), whole((width, chan)), whole((heads, chan))],
-        out_specs=[pl.BlockSpec((BLOCK, chan), lambda i: (i, 0)), pl.BlockSpec((BLOCK // tok * heads, tok), lambda i: (i, 0))],
-        out_shape=[jax.ShapeDtypeStruct((rows, chan), BF16), jax.ShapeDtypeStruct((rows // tok * heads, tok), F32)],
+        in_specs=[row_spec, whole((chan, 2 * width)), whole((width, chan)), whole((heads, chan)), whole(s_rows.shape)],
+        out_specs=[row_spec, pl.BlockSpec((BLOCK // tok * heads, tok), lambda i: (i, 0)), row_spec, whole((PLANE,) + s_rows.shape)],
+        out_shape=[jax.ShapeDtypeStruct((rows, chan), BF16), jax.ShapeDtypeStruct((rows // tok * heads, tok), F32), jax.ShapeDtypeStruct((rows, chan), BF16), jax.ShapeDtypeStruct((PLANE,) + s_rows.shape, BF16)],
+        scratch_shapes=[pltpu.VMEM((PLANE,) + s_rows.shape, BF16), pltpu.SemaphoreType.DMA, pltpu.SemaphoreType.DMA],
+        compiler_params=pltpu.CompilerParams(collective_id=0, has_side_effects=True),
         name="pair_forward",
         cost_estimate=pl.CostEstimate(flops=6 * rows * chan * width, bytes_accessed=4 * rows * chan, transcendentals=0),
-    )(z_rows, w_ab, w_po, w_bias_t)
-
-
-def pair_backward_kernel(z_ref, zn_ref, dz_ref, gl_ref, w_ab_ref, w_ab_t_ref, w_po_t_ref, w_bias_t_ref, dzi_ref, dwab_ref, dwpo_t_ref, dwb_t_ref):
+    )(z_rows, w_ab, w_po, w_bias_t, s_rows)
+
+
+def pair_backward_kernel(z_ref, zn_ref, dz_ref, gl_ref, w_ab_ref, w_ab_t_ref, w_po_t_ref, w_bias_t_ref, dzi_ref, dwab_ref, dwpo_t_ref):
     width = w_po_t_ref.shape[1]
     heads = w_bias_t_ref.shape[0]
 
@@ -99,12 +166,10 @@
     def _():
         dwab_ref[...] = jnp.zeros_like(dwab_ref)
         dwpo_t_ref[...] = jnp.zeros_like(dwpo_t_ref)
-        dwb_t_ref[...] = jnp.zeros_like(dwb_t_ref)
 
     bias_norm, bias_inv = layer_norm(zn_ref[...])
     groups = gl_ref.shape[0] // heads
     gl = jnp.concatenate([gl_ref[k * heads:(k + 1) * heads, :] for k in range(groups)], axis=1)
-    dwb_t_ref[...] += mm(gl, bias_norm.astype(BF16))
     grad_norm = mm_tn(gl, w_bias_t_ref[...])
     grad_new = dz_ref[...].astype(F32) + norm_grad(bias_norm, bias_inv, grad_norm)
     grad_new_bf = grad_new.astype(BF16)
@@ -130,20 +195,28 @@
         pair_backward_kernel,
         grid=(rows // BLOCK,),
         in_specs=[row_spec, row_spec, row_spec, pl.BlockSpec((BLOCK // tok * heads, tok), lambda i: (i, 0)), whole((chan, 2 * width)), whole((2 * width, chan)), whole((chan, width)), whole((heads, chan))],
-        out_specs=[row_spec, whole((chan, 2 * width)), whole((chan, width)), whole((heads, chan))],
-        out_shape=[jax.ShapeDtypeStruct((rows, chan), BF16), jax.ShapeDtypeStruct((chan, 2 * width), F32), jax.ShapeDtypeStruct((chan, width), F32), jax.ShapeDtypeStruct((heads, chan), F32)],
+        out_specs=[row_spec, whole((chan, 2 * width)), whole((chan, width))],
+        out_shape=[jax.ShapeDtypeStruct((rows, chan), BF16), jax.ShapeDtypeStruct((chan, 2 * width), F32), jax.ShapeDtypeStruct((chan, width), F32)],
         name="pair_backward",
         cost_estimate=pl.CostEstimate(flops=16 * rows * chan * width, bytes_accessed=8 * rows * chan, transcendentals=0),
     )(z_rows, z_new, dz_rows, grad_logits, w_ab, w_ab_t, w_po_t, w_bias_t)
 
 
-def single_kernel(tok, s_all_ref, s_ref, ds_ref, mask_ref, bias_ref, w_q_ref, q_bias_ref, w_kv_ref, w_g_ref, w_o_ref, w_sa_ref, w_sb_ref, w_so_ref,
-                  gl_ref, part_ref, gact_ref, gmid_ref, dwq_ref, dqb_ref, dwkv_ref, dwg_ref, dwo_ref, dwsa_ref, dwsb_ref, dwso_ref,
-                  q_exp, g_exp, prob, gkv):
+def put(ref, offset, matrix):
+    rows, cols = matrix.shape
+    for j in range(cols // LANES):
+        ref[offset + j * rows:offset + (j + 1) * rows, :] = matrix[:, j * LANES:(j + 1) * LANES].astype(BF16)
+    return offset + cols // LANES * rows
+
+
+def single_kernel(tok, s_all_ref, s_ref, ds_ref, mask_ref, bias_ref, bias_norm_ref, w_q_ref, q_bias_ref, w_kv_ref, w_g_ref, w_o_ref, w_sa_ref, w_sb_ref, w_so_ref,
+                  gl_ref, part_ref, gact_ref, gmid_ref, wide_ref, attn_ref,
+                  q_exp, g_exp, prob, gkv, stage):
     rows, chan = s_ref.shape
-    num_cplx = s_all_ref.shape[0] // tok
+    num_cplx = s_all_ref.shape[0] * rows // tok
+    row_count = rows // num_cplx
     heads = bias_ref.shape[0] // rows
-    per = rows // num_cplx * heads
+    per = row_count * heads
     scale = HEAD_DIM ** -0.5
     flat = rows * heads
 
@@ -160,8 +233,9 @@
         kept = jnp.where(head_mask(values.shape[0]), values, 0.0)
         return jnp.sum(kept.reshape(values.shape[0] // heads, heads, chan), axis=1)
 
-    a_all, _ = layer_norm(s_all_ref[...])
-    a_all = a_all.astype(BF16)
+    a_wide, _ = layer_norm(s_all_ref[...])
+    a_wide = jnp.concatenate([a_wide[:, b * row_count:(b + 1) * row_count, :].reshape(tok, chan) for b in range(num_cplx)], axis=0)
+    a_all = a_wide.astype(BF16)
     kv = mm(a_all, w_kv_ref[...]).astype(BF16)
     s_wide = s_ref[...].astype(F32)
     s_norm, _ = layer_norm(s_wide)
@@ -191,19 +265,19 @@
     hidden, grad_ta, grad_tb = swiglu_and_grad(trans_a, trans_b, grad_hidden)
     grad_ta = grad_ta.astype(BF16)
     grad_tb = grad_tb.astype(BF16)
-    dwso_ref[...] = mm_tn(hidden.astype(BF16), ds_rows)
-    dwsa_ref[...] = mm_tn(mid_act, grad_ta)
-    dwsb_ref[...] = mm_tn(mid_act, grad_tb)
+    at = put(wide_ref, 0, mm_tn(mid_act, grad_ta))
+    at = put(wide_ref, at, mm_tn(mid_act, grad_tb))
+    put(wide_ref, at, mm_tn(hidden.astype(BF16), ds_rows))
     grad_mid_norm = mm_nt(grad_ta, w_sa_ref[...]) + mm_nt(grad_tb, w_sb_ref[...])
     grad_mid = ds_rows.astype(F32) + norm_grad(mid_norm, mid_inv, grad_mid_norm)
     grad_mid_bf = grad_mid.astype(BF16)
     gmid_ref[...] = grad_mid
-    dwo_ref[...] = mm_tn(gated, grad_mid_bf)
     grad_gated = mm_nt(grad_mid_bf, w_o_ref[...])
     grad_gate = (grad_gated * attended * gate * (1.0 - gate)).astype(BF16)
     grad_att = (grad_gated * gate).astype(BF16)
     g_exp[...] = jnp.where(head_mask(flat), expand(grad_att), 0.0).astype(BF16)
     grad_query = []
+    grad_w_bias = jnp.zeros((heads, bias_norm_ref.shape[1]), F32)
     for b in range(num_cplx):
         keys = kv[b * tok:(b + 1) * tok, :chan]
         vals = kv[b * tok:(b + 1) * tok, chan:]
@@ -212,33 +286,240 @@
         grad_prob = mm_nt(g_rows, vals)
         grad_logits = (p_wide * (grad_prob - jnp.sum(p_wide * grad_prob, axis=-1, keepdims=True))).astype(BF16)
         gl_ref[b * per:(b + 1) * per, :] = grad_logits
+        gl_wide = jnp.concatenate([grad_logits[i * heads:(i + 1) * heads, :] for i in range(row_count)], axis=1)
+        grad_w_bias = grad_w_bias + mm(gl_wide, bias_norm_ref[b * row_count * tok:(b + 1) * row_count * tok, :])
         grad_query.append(fold(mm(grad_logits, keys)) * scale)
         gkv[b * tok:(b + 1) * tok, :chan] = (mm_tn(grad_logits, q_exp[b * per:(b + 1) * per, :]) * scale).astype(BF16)
         gkv[b * tok:(b + 1) * tok, chan:] = mm_tn(p_wide.astype(BF16), g_rows).astype(BF16)
     grad_query = jnp.concatenate(grad_query, axis=0)
     grad_query_bf = grad_query.astype(BF16)
-    dwkv_ref[...] = mm_tn(a_all, gkv[...])
-    part_ref[...] = mm_nt(gkv[...], w_kv_ref[...]).astype(BF16)
-    dwq_ref[...] = mm_tn(act, grad_query_bf)
-    dqb_ref[...] = jnp.sum(grad_query, axis=0, keepdims=True)
-    dwg_ref[...] = mm_tn(act, grad_gate)
+    at = put(attn_ref, 0, mm_tn(act, grad_query_bf))
+    at = put(attn_ref, at, mm_tn(a_all, gkv[...]))
+    at = put(attn_ref, at, mm_tn(act, grad_gate))
+    at = put(attn_ref, at, mm_tn(gated, grad_mid_bf))
+    at = put(attn_ref, at, grad_w_bias)
+    grad_q_bias = jnp.sum(grad_query, axis=0, keepdims=True)
+    line = lax.broadcasted_iota(jnp.int32, (heads, LANES), 0)
+    lines = jnp.zeros((heads, LANES), F32)
+    for j in range(chan // LANES):
+        lines = jnp.where(line == j, grad_q_bias[:, j * LANES:(j + 1) * LANES], lines)
+    at = put(attn_ref, at, lines)
+    attn_ref[at:, :] = jnp.zeros((attn_ref.shape[0] - at, LANES), BF16)
+    part = mm_nt(gkv[...], w_kv_ref[...])
+    for b in range(num_cplx):
+        stage[:, b * row_count:(b + 1) * row_count, :] = part[b * tok:(b + 1) * tok, :].reshape(tok // row_count, row_count, chan)
+    part_ref[...] = stage[...].astype(BF16)
     gact_ref[...] = mm_nt(grad_query_bf, w_q_ref[...]) + mm_nt(grad_gate, w_g_ref[...])
 
 
-def single_track(tok, s_all, s_rows, ds_rows, mask, bias, weights):
+def single_track(tok, s_all, s_rows, ds_rows, mask, bias, bias_norm, weights):
     rows, chan = s_rows.shape
     flat = bias.shape[0]
-    all_rows = s_all.shape[0]
-    shapes = [((flat, tok), BF16), ((all_rows, chan), BF16), ((rows, chan), F32), ((rows, chan), F32)] + [(w.shape, F32) for w in weights]
+    all_rows = PLANE * rows
+    shapes = [((flat, tok), BF16), (s_all.shape, BF16), ((rows, chan), F32), ((rows, chan), F32), ((SHARDS * PIECE_ROWS[0], LANES), BF16), ((SHARDS * PIECE_ROWS[1], LANES), BF16)]
     return pl.pallas_call(
         functools.partial(single_kernel, tok),
         out_shape=[jax.ShapeDtypeStruct(*s) for s in shapes],
-        in_specs=[pl.BlockSpec(memory_space=pltpu.VMEM)] * (5 + len(weights)),
+        in_specs=[pl.BlockSpec(memory_space=pltpu.VMEM)] * (6 + len(weights)),
         out_specs=[pl.BlockSpec(memory_space=pltpu.VMEM)] * len(shapes),
-        scratch_shapes=[pltpu.VMEM((flat, chan), BF16), pltpu.VMEM((flat, chan), BF16), pltpu.VMEM((flat, tok), F32), pltpu.VMEM((all_rows, 2 * chan), BF16)],
+        scratch_shapes=[pltpu.VMEM((flat, chan), BF16), pltpu.VMEM((flat, chan), BF16), pltpu.VMEM((flat, tok), F32), pltpu.VMEM((all_rows, 2 * chan), BF16), pltpu.VMEM(s_all.shape, F32)],
         name="single_track",
         cost_estimate=pl.CostEstimate(flops=3 * 10**9, bytes_accessed=20 * 2**20, transcendentals=0),
-    )(s_all, s_rows, ds_rows, mask, bias, *weights)
+    )(s_all, s_rows, ds_rows, mask, bias, bias_norm, *weights)
+
+
+class Piece:
+    def __init__(self, here, rows, whole, got, half, got_one, quarter, got_two, cross, total, send_sem, recv_sem):
+        self.here, self.rows = here, rows
+        self.whole, self.got, self.half = whole, got, half
+        self.got_one, self.quarter, self.got_two = got_one, quarter, got_two
+        self.cross, self.total = cross, total
+        self.send_sem, self.recv_sem = send_sem, recv_sem
+
+    def cut(self, ref, index, count=1):
+        start = index * self.rows
+        if not isinstance(start, int):
+            start = pl.multiple_of(start, 16)
+        return ref.at[pl.ds(start, count * self.rows)]
+
+    def mine(self, route):
+        return self.here['core'] * (SHARDS // 2) + route * PLANE
+
+    def fan_out(self, phase, route, axis, src, dst):
+        for k in range(1, SIDE):
+            send(src(k), dst(k), self.send_sem.at[phase], self.recv_sem.at[phase, route], neighbour(self.here, axis, k))
+
+    def swap_in(self, route):
+        other = (1 - self.here['core']) * (SHARDS // 2) + route * PLANE
+        send(self.cut(self.whole, other, PLANE), self.cut(self.got, route * PLANE, PLANE), self.send_sem.at[0], self.recv_sem.at[0, route], partner(self.here))
+
+    def scatter_one(self, route):
+        axis = ROUTES[route][0]
+        spot = route * PLANE
+        got = self.cut(self.got, spot, PLANE)
+        wait_bytes(got, self.recv_sem.at[0, route])
+        own = self.cut(self.whole, self.mine(route), PLANE)
+        self.cut(self.half, spot, PLANE)[...] = (own[...].astype(F32) + got[...].astype(F32)).astype(BF16)
+        self.fan_out(1, route, axis,
+                     lambda k: self.cut(self.half, spot + (self.here[axis] + k) % SIDE * SIDE, SIDE),
+                     lambda k: self.cut(self.got_one, (route * 3 + k - 1) * SIDE, SIDE))
+
+    def scatter_two(self, route):
+        first, axis = ROUTES[route][0], ROUTES[route][1]
+        wait_bytes(self.cut(self.got_one, route * 3 * SIDE, 3 * SIDE), self.recv_sem.at[1, route])
+        total = self.cut(self.half, route * PLANE + self.here[first] * SIDE, SIDE)[...].astype(F32)
+        for k in range(3):
+            total = total + self.cut(self.got_one, (route * 3 + k) * SIDE, SIDE)[...].astype(F32)
+        self.cut(self.quarter, route * SIDE, SIDE)[...] = total.astype(BF16)
+        self.fan_out(2, route, axis,
+                     lambda k: self.cut(self.quarter, route * SIDE + (self.here[axis] + k) % SIDE),
+                     lambda k: self.cut(self.got_two, route * 3 + k - 1))
+
+    def exchange(self, route):
+        second, axis = ROUTES[route][1], ROUTES[route][2]
+        wait_bytes(self.cut(self.got_two, route * 3, 3), self.recv_sem.at[2, route])
+        total = self.cut(self.quarter, route * SIDE + self.here[second])[...].astype(F32)
+        for k in range(3):
+            total = total + self.cut(self.got_two, route * 3 + k)[...].astype(F32)
+        slot = self.cut(self.cross, route * SIDE + self.here[axis])
+        slot[...] = total.astype(BF16)
+        self.fan_out(3, route, axis, lambda k: slot, lambda k: slot)
+
+    def gather_two(self, route):
+        first, axis = ROUTES[route][0], ROUTES[route][1]
+        wait_bytes(self.cut(self.got_two, route * 3, 3), self.recv_sem.at[3, route])
+        total = self.cut(self.cross, route * SIDE)[...].astype(F32)
+        for k in range(1, SIDE):
+            total = total + self.cut(self.cross, route * SIDE + k)[...].astype(F32)
+        shard = self.cut(self.total, self.mine(route) + self.here[first] * SIDE + self.here[axis])
+        shard[...] = total.astype(BF16)
+        self.fan_out(4, route, axis, lambda k: shard, lambda k: shard)
+
+    def gather_one(self, route):
+        axis = ROUTES[route][0]
+        wait_bytes(self.cut(self.got_two, route * 3, 3), self.recv_sem.at[4, route])
+        group = self.cut(self.total, self.mine(route) + self.here[axis] * SIDE, SIDE)
+        self.fan_out(5, route, axis, lambda k: group, lambda k: group)
+
+    def swap_out(self, route):
+        wait_bytes(self.cut(self.got_one, route * 3 * SIDE, 3 * SIDE), self.recv_sem.at[5, route])
+        own = self.cut(self.total, self.mine(route), PLANE)
+        send(own, own, self.send_sem.at[6], self.recv_sem.at[6, route], partner(self.here))
+
+    def finish(self, route):
+        wait_bytes(self.cut(self.got, route * PLANE, PLANE), self.recv_sem.at[6, route])
+
+    def drain(self):
+        for phase, like in enumerate((self.got, self.got_one, self.got_two, self.got_two, self.got_two, self.got_one, self.got)):
+            wait_bytes(like, self.send_sem.at[phase])
+
+    STAGES = ('swap_in', 'scatter_one', 'scatter_two', 'exchange', 'gather_two', 'gather_one', 'swap_out', 'finish')
+
+    def stage(self, number):
+        for route in range(3):
+            getattr(self, self.STAGES[number])(route)
+
+
+def piece_scratch(rows):
+    buffer = lambda shards: pltpu.VMEM((shards * rows, LANES), BF16)
+    return [buffer(48), buffer(48), buffer(36), buffer(12), buffer(9), buffer(12), pltpu.SemaphoreType.DMA((7,)), pltpu.SemaphoreType.DMA((7, 3))]
+
+
+def reduce_kernel(*refs):
+    here = position()
+    wholes, part_ref, outs, sum_ref = refs[:3], refs[3], refs[4:7], refs[7]
+    part_got, part_send, part_recv, out_sem = refs[8:12]
+    totals = refs[12:15]
+    pieces = []
+    for n in range(3):
+        scratch = refs[15 + 8 * n:23 + 8 * n]
+        pieces.append(Piece(here, PIECE_ROWS[n], wholes[n], *scratch[:6], totals[n], *scratch[6:]))
+    meet([neighbour(here, 'x', k) for k in range(1, SIDE)] + [plane_member(here, k) for k in range(1, PLANE)] + [partner(here)])
+    for piece in pieces:
+        piece.stage(0)
+    for piece in pieces:
+        piece.stage(1)
+    for k in range(1, PLANE):
+        send(part_ref.at[(here['dap'] + k) % PLANE], part_got.at[k - 1], part_send, part_recv, plane_member(here, k))
+    for number in range(2, 8):
+        for piece in pieces:
+            piece.stage(number)
+    wait_bytes(part_got, part_recv)
+    total = part_ref[here['dap']].astype(F32)
+    for k in range(PLANE - 1):
+        total = total + part_got[k].astype(F32)
+    sum_ref[...] = total
+    wait_bytes(part_got, part_send)
+    copies = [pltpu.make_async_copy(totals[n], outs[n], out_sem.at[n]) for n in range(3)]
+    for copy in copies:
+        copy.start()
+    for piece in pieces:
+        piece.drain()
+    for copy in copies:
+        copy.wait()
+
+
+def reduce_all(wholes, part):
+    vmem = pl.BlockSpec(memory_space=pltpu.VMEM)
+    shapes = [jax.ShapeDtypeStruct(w.shape, BF16) for w in wholes] + [jax.ShapeDtypeStruct(part.shape[1:], F32)]
+    scratch = [pltpu.VMEM((PLANE - 1,) + part.shape[1:], BF16), pltpu.SemaphoreType.DMA, pltpu.SemaphoreType.DMA, pltpu.SemaphoreType.DMA((3,))]
+    scratch = scratch + [pltpu.VMEM(w.shape, BF16) for w in wholes]
+    for rows in PIECE_ROWS:
+        scratch = scratch + piece_scratch(rows)
+    return pl.pallas_call(
+        reduce_kernel,
+        out_shape=shapes,
+        in_specs=[vmem] * 4,
+        out_specs=[pl.BlockSpec(memory_space=pl.ANY)] * 3 + [vmem],
+        scratch_shapes=scratch,
+        compiler_params=pltpu.CompilerParams(collective_id=1, has_side_effects=True),
+        name="reduce_all",
+        cost_estimate=pl.CostEstimate(flops=10**9, bytes_accessed=20 * 2**20, transcendentals=0),
+    )(*wholes, part)
+
+
+LAYOUT = (('w_sa', 0, 0, 384, 1536), ('w_sb', 0, 4608, 384, 1536), ('w_so', 0, 9216, 1536, 384),
+          ('w_q', 1, 0, 384, 384), ('w_kv', 1, 1152, 384, 768), ('w_g', 1, 3456, 384, 384), ('w_o', 1, 4608, 384, 384),
+          ('w_pa', 2, 0, 128, 512), ('w_pb', 2, 512, 128, 512), ('w_po_t', 2, 1024, 128, 512))
+
+
+def unpack_kernel(*refs):
+    totals, outs, stages, sems = refs[:3], refs[3:15], refs[15:27], refs[27]
+    copies = []
+    for n, (name, piece, offset, rows, cols) in enumerate(LAYOUT):
+        blocks = [totals[piece][offset + j * rows:offset + (j + 1) * rows, :].astype(F32) for j in range(cols // LANES)]
+        if name == 'w_po_t':
+            for j, block in enumerate(blocks):
+                stages[n][j * LANES:(j + 1) * LANES, :] = block.T
+        else:
+            for j, block in enumerate(blocks):
+                stages[n][:, j * LANES:(j + 1) * LANES] = block
+        copies.append(pltpu.make_async_copy(stages[n], outs[n], sems.at[n]))
+        copies[-1].start()
+    stages[10][...] = totals[1][5760:5776, :].astype(F32)
+    lines = totals[1][5776:5792, :].astype(F32)
+    for j in range(3):
+        stages[11][:, j * LANES:(j + 1) * LANES] = lines[j:j + 1, :]
+    for n in (10, 11):
+        copies.append(pltpu.make_async_copy(stages[n], outs[n], sems.at[n]))
+        copies[-1].start()
+    for copy in copies:
+        copy.wait()
+
+
+def unpack(totals):
+    shapes = [(cols, rows) if name == 'w_po_t' else (rows, cols) for name, _, _, rows, cols in LAYOUT] + [(16, 128), (1, 384)]
+    outs = pl.pallas_call(
+        unpack_kernel,
+        out_shape=[jax.ShapeDtypeStruct(shape, F32) for shape in shapes],
+        in_specs=[pl.BlockSpec(memory_space=pltpu.VMEM)] * 3,
+        out_specs=[pl.BlockSpec(memory_space=pl.ANY)] * 12,
+        scratch_shapes=[pltpu.VMEM(shape, F32) for shape in shapes] + [pltpu.SemaphoreType.DMA((12,))],
+        name="unpack",
+        cost_estimate=pl.CostEstimate(flops=10**7, bytes_accessed=16 * 2**20, transcendentals=0),
+    )(*totals)
+    names = [entry[0] for entry in LAYOUT] + ['w_bias_t', 'q_bias']
+    return dict(zip(names, outs))
 
 
 def solution(mesh):
@@ -254,19 +535,17 @@
         w_bias_t = w_bias.T
         z_rows = pair_z.reshape(-1, pair_dim)
         dz_rows = dz_out.reshape(-1, pair_dim)
-        s_all = lax.all_gather(single_s, 'dap', axis=1, tiled=True).reshape(-1, chan)
-        z_new, bias = pair_forward(z_rows, w_ab, w_po, w_bias_t, tok)
         s_rows = single_s.reshape(-1, chan)
-        outs = single_track(tok, s_all, s_rows, ds_out.reshape(-1, chan), token_mask, bias, (w_q, q_bias[None], w_kv, w_g, w_o, w_sa, w_sb, w_so))
-        grad_logits, part, gact, gmid = outs[:4]
-        dwq, dqb, dwkv, dwg, dwo, dwsa, dwsb, dwso = outs[4:]
-        part_sum = lax.psum_scatter(part.reshape(num_cplx, -1, chan), 'dap', scatter_dimension=1, tiled=True)
+        z_new, bias, bias_norm, s_all = pair_forward(z_rows, w_ab, w_po, w_bias_t, s_rows, tok)
+        grad_logits, part, gact, gmid, wide, attn = single_track(tok, s_all, s_rows, ds_out.reshape(-1, chan), token_mask, bias, bias_norm, (w_q, q_bias[None], w_kv, w_g, w_o, w_sa, w_sb, w_so))
+        dz_in, dwab, dwpo_t = pair_backward(z_rows, z_new, dz_rows, grad_logits, w_ab, w_ab_t, w_po.T, w_bias_t, tok)
+        pair = jnp.concatenate([dwab.reshape(pair_dim, -1, LANES), dwpo_t.reshape(pair_dim, -1, LANES)], axis=1).transpose(1, 0, 2).reshape(-1, LANES).astype(BF16)
+        *totals, part_sum = reduce_all((wide, attn, pair), part)
         s_norm, s_inv = layer_norm(s_rows)
-        ds_in = (gmid + norm_grad(s_norm, s_inv, gact + part_sum.reshape(-1, chan).astype(F32))).astype(BF16)
-        dz_in, dwab, dwpo_t, dwb_t = pair_backward(z_rows, z_new, dz_rows, grad_logits, w_ab, w_ab_t, w_po.T, w_bias_t, tok)
-        grads = (dwab[:, :width], dwab[:, width:], dwpo_t.T, dwb_t.T, dwq, dqb[0], dwkv, dwg, dwo, dwsa, dwsb, dwso)
-        grads = lax.psum(grads, ('dap', 'dp'))
-        return (dz_in.reshape(pair_z.shape), ds_in.reshape(single_s.shape)) + tuple(grads)
+        ds_in = (gmid + norm_grad(s_norm, s_inv, gact + part_sum)).astype(BF16)
+        grads = unpack(totals)
+        ordered = (grads['w_pa'], grads['w_pb'], grads['w_po_t'], grads['w_bias_t'].T, grads['w_q'], grads['q_bias'][0], grads['w_kv'], grads['w_g'], grads['w_o'], grads['w_sa'], grads['w_sb'], grads['w_so'])
+        return (dz_in.reshape(pair_z.shape), ds_in.reshape(single_s.shape)) + ordered
 
     in_specs = (pair_spec, single_spec, P('dp', None), pair_spec, single_spec) + (P(),) * 12
     out_specs = (pair_spec, single_spec) + (P(),) * 12

time: 349 us -> 128 us (0.37)
  waiting for transfers between devices: 169 us -> 0 us
  blocking collectives: 91.5 us -> 0 us
  Pallas kernels: 44.3 us -> 113 us
  local copies, waits for them, and re-layouts: 24.6 us -> 6 us
  between operations: 14.8 us -> 0.72 us
  other arithmetic: 3.4 us -> 8.28 us
    psum x1 -> x0, waiting for transfers between devices: 169 us -> none  [body(): grads = lax.psum(grads, ('dap', 'dp'))]
    pallas_call x1 -> x3, Pallas kernels: 11.2 us -> 82 us  [the longest x1 56.1 us: reduce_all(): pl.pallas_call(reduce_kernel, out_shape=shapes, in_specs=[vmem] * 4, out_...]
    psum x1 -> x0, blocking collectives: 69.2 us -> none  [body(): grads = lax.psum(grads, ('dap', 'dp'))]
    all_gather x1 -> x0, blocking collectives: 22.3 us -> none  [body(): lax.all_gather(single_s, 'dap', axis=1, tiled=True).reshape(-1, chan)]
    unnamed x40 -> x9, local copies, waits for them, and re-layouts: 20.4 us -> 3.73 us
  transfers between devices with their start and end apart: 2 -> 0, of which waited for: 1 -> 0; matrix products, arithmetic and copies ran while one was open for 2% -> 0% of each run, Pallas kernels for 5% -> 0%
where the time goes in v2:
time: 128 us
  Pallas kernels  113 us (88%)
  other arithmetic  8.28 us (6%)
  local copies, waits for them, and re-layouts  6 us (5%)
    pallas_call x1, Pallas kernels, reduce_all(): pl.pallas_call(reduce_kernel, out_shape=shapes, in_specs=[vmem] * 4, out_...  56.1 us
    pallas_call x1, Pallas kernels, pair_forward(): pl.pallas_call(pair_forward_kernel, grid=(rows // BLOCK,), in_specs=[row_...  19 us
    pallas_call x1, Pallas kernels, pair_backward(): pl.pallas_call(pair_backward_kernel, grid=(rows // BLOCK,), in_specs=[row...  18.2 us
    pallas_call x1, Pallas kernels, single_track(): pl.pallas_call(functools.partial(single_kernel, tok), out_shape=[jax.Shap...  12.6 us
    pallas_call x1, Pallas kernels, unpack(): pl.pallas_call(unpack_kernel, out_shape=[jax.ShapeDtypeStruct(shape, F32)...  6.94 us
    unnamed x9, local copies, waits for them, and re-layouts  3.73 us

profile of v2, /device:TPU:1, one launch (start us, length us, event | category | flops | bytes accessed | tf_op | source)
XLA Modules:
  0.0 127.8 jit_solution(8539769954557497281)
XLA Ops:
  0.6 1.2 broadcast_in_dim.2.q_bias_ref
  1.9 0.8 convert_reduce_fusion
  2.7 0.1 div.17
  2.8 0.9 fusion.1
  3.7 0.1 rsqrt.12
  3.8 1.0 copy.31
  4.8 1.0 copy.32
  5.9 1.7 %copy.34 = bf16[512,128]{0,1:T(8,128)(2,1)} copy(bf16[512,128]{1,0:T(8,128)(2,1)} %w_po_ref.1) | data formatting | bytes 262144 | tf_op args[7]
  7.5 0.7 fusion.3
  8.3 0.8 copy.33.w_ab_ref
  9.1 19.0 %pair_forward.1 = (bf16[4096,128]{1,0:T(8,128)(2,1)}, f32[512,128]{1,0:T(8,128)}, bf16[4096,128]{1,0:T(8,128)(2,1)}, bf16[16,32,384]{2,1,0:T(8,128)(2,1)}) custom-call(bf16[4096,128]{1,0:T(8,128)(2,1)} %bitcast.31, bf16[128,1024]{1,0:T(8,128)(2,1)} %copy.33.w_ab_ref, bf16[512,128]{1,0:T(8,128)(2,1)} %w_po_ref.1, bf16[16,128]{1,0:T(8,128)(2,1)} %bitcast.36, ...), custom_call_target="tpu_custom_call" | custom-call | flops 1610612736 | bytes 2097152 | tf_op jit(solution)/shard_map/pair_forward/pallas_call | solution.py:148
  28.1 12.6 %single_track.1 = (bf16[512,128]{1,0:T(8,128)(2,1)}, bf16[16,32,384]{2,1,0:T(8,128)(2,1)}, f32[32,384]{1,0:T(8,128)}, f32[32,384]{1,0:T(8,128)}, bf16[13824,128]{1,0:T(8,128)(2,1)}, /*index=5*/bf16[6144,128]{1,0:T(8,128)(2,1)}) custom-call(bf16[16,32,384]{2,1,0:T(8,128)(2,1)} %get-tuple-element.44.s_all_ref, bf16[32,384]{1,0:T(8,128)(2,1)} %bitcast.29, ...), custom_call_target="tpu_custom_call" | custom-call | flops 3000000000 | bytes 20971520 | tf_op jit(solution)/shard_map/single_track/pallas_call | solution.py:320
  40.7 18.2 %pair_backward.1 = (bf16[4096,128]{1,0:T(8,128)(2,1)}, f32[128,1024]{1,0:T(8,128)}, f32[128,512]{1,0:T(8,128)}) custom-call(bf16[4096,128]{1,0:T(8,128)(2,1)} %bitcast.32, bf16[4096,128]{1,0:T(8,128)(2,1)} %get-tuple-element.43.zn_ref, bf16[4096,128]{1,0:T(8,128)(2,1)} %bitcast.33, bf16[512,128]{1,0:T(8,128)(2,1)} %get-tuple-element.47.gl_ref, ...), custom_call_target="tpu_custom_call" | custom-call | flops 4294967296 | bytes 4194304 | tf_op jit(solution)/shard_map/pair_backward/pallas_call | solution.py:194
  58.9 1.0 copy_bitcast_fusion.1
  59.9 1.1 copy_bitcast_fusion
  61.0 0.8 pad_maximum_fusion
  61.8 0.0 copy-start
  61.8 0.0 copy-start.2
  61.8 0.0 copy-start.1
  61.8 56.1 %reduce_all.1 = (bf16[13824,128]{1,0:T(8,128)(2,1)}, bf16[6144,128]{1,0:T(8,128)(2,1)}, bf16[1536,128]{1,0:T(8,128)(2,1)}, f32[32,384]{1,0:T(8,128)}) custom-call(bf16[13824,128]{1,0:T(8,128)(2,1)} %get-tuple-element.51.refs_0_, bf16[6144,128]{1,0:T(8,128)(2,1)} %get-tuple-element.52.refs_1_, bf16[1536,128]{1,0:T(8,128)(2,1)} %bitcast.27, ...), custom_call_target="tpu_custom_call" | custom-call | flops 1000000000 | bytes 20971520 | tf_op jit(solution)/shard_map/reduce_all/pallas_call | solution.py:469
  117.8 0.0 copy-done
  117.9 0.0 copy-done.2
  117.9 1.0 fusion.4
  118.9 0.0 copy-done.1
  118.9 0.7 fusion.2
  119.6 6.9 %unpack.1 = (f32[384,1536]{1,0:T(8,128)}, f32[384,1536]{1,0:T(8,128)}, f32[1536,384]{1,0:T(8,128)}, f32[384,384]{1,0:T(8,128)}, f32[384,768]{1,0:T(8,128)}, /*in...) custom-call(bf16[13824,128]{1,0:T(8,128)(2,1)} %get-tuple-element.57, ...), custom_call_target="tpu_custom_call" | custom-call | flops 10000000 | bytes 16777216 | tf_op jit(solution)/shard_map/unpack/pallas_call | solution.py:512
  126.5 1.3 reduce.2
  (3 shorter events, 0.0 us)
Async XLA Ops:
  61.8 56.1 %copy-start = (bf16[4,8,384]{2,1,0:T(8,128)(2,1)S(1)}, bf16[4,8,384]{2,1,0:T(8,128)(2,1)}, u32[]{:S(2)}) copy-start(bf16[4,8,384]{2,1,0:T(8,128)(2,1)} %param.18) | copy-start | bytes 73732
  61.8 56.1 %copy-start.2 = (f32[32,384]{1,0:T(8,128)S(1)}, f32[32,384]{1,0:T(8,128)}, u32[]{:S(2)}) copy-start(f32[32,384]{1,0:T(8,128)} %get-tuple-element.50) | copy-start | bytes 147460
  61.8 57.1 %copy-start.1 = (f32[32,384]{1,0:T(8,128)S(1)}, f32[32,384]{1,0:T(8,128)}, u32[]{:S(2)}) copy-start(f32[32,384]{1,0:T(8,128)} %get-tuple-element.49) | copy-start | bytes 147460
